TPU v7x, 32 devices: a whole 2x2x4 slice. The times are simulated.
32 devices in a mesh: row: 4 (over y, x), col: 8 (over z, core).
Axes of the slice: x: 2, y: 2, z: 4, core: 2. Of those that a mesh axis runs over, the one named last changes fastest.
Arguments:
- hidden_states: bfloat16 [1536, 4096], P('col', 'row'), may hold values from -50 to 50
- out_grad: bfloat16 [1536, 4096], P('col', 'row'), may hold values from -6 to 6
- lengths: int32 [4, 4], P('row'), may hold values from 1 to 512, 1024 in all within a row
- norm_gains: bfloat16 [2, 2, 1536], P(None, None, 'col'), may hold values from 0.099609375 to 1.8984375
- qkv_weight: bfloat16 [2, 1536, 2048], P(None, 'row', 'col'), may hold values from -0.15625 to 0.15625
- qkv_bias: bfloat16 [2, 16, 128], P(None, 'col', 'row'), may hold values from -2 to 2
- out_weight: bfloat16 [2, 1536, 1536], P(None, 'col', 'row'), may hold values from -0.625 to 0.625
- gate_weight: bfloat16 [2, 1536, 8960], P(None, 'row', 'col'), may hold values from -0.15625 to 0.15625
- up_weight: bfloat16 [2, 1536, 8960], P(None, 'row', 'col'), may hold values from -0.15625 to 0.15625
- down_weight: bfloat16 [2, 8960, 1536], P(None, 'col', 'row'), may hold values from -0.0625 to 0.0625
Outputs:
- out_states: bfloat16 [1536, 4096], P('col', 'row')
- input_grad: float32 [1536, 4096], P('col', 'row')
- norm_gains_grad: float32 [2, 2, 1536], P(None, None, 'col')
- qkv_weight_grad: float32 [2, 1536, 2048], P(None, 'row', 'col')
- qkv_bias_grad: float32 [2, 16, 128], P(None, 'col', 'row')
- out_weight_grad: float32 [2, 1536, 1536], P(None, 'col', 'row')
- gate_weight_grad: float32 [2, 1536, 8960], P(None, 'row', 'col')
- up_weight_grad: float32 [2, 1536, 8960], P(None, 'row', 'col')
- down_weight_grad: float32 [2, 8960, 1536], P(None, 'col', 'row')
Inputs may be any that keep to these rules, and one draw needn't show every extreme that they name: Row g lists, in order, the lengths of the sequences packed into row group g; each row sums to 1024 and holds one length of exactly 512.
All inputs are finite; a program needn't handle non-finite values.
Results may differ from a plain program's by a relative error of at most 0.017.
Values may be sent and summed in bfloat16 or wider, within the bound.
A program may use at most 256 MiB of HBM per device.

v0:
```python
from functools import partial
import jax
import jax.numpy as jnp
from jax import lax
from jax.sharding import PartitionSpec as P

D = 1536
HEADS = 12
KV_HEADS = 2
HD = 128
LAYERS = 2
SEQ_MAX = 512
QB = 128
eps_norm = 1e-06
rope_base = 1000000.0
neg_fill = -1e30


def row_starts(sizes, count):
    ends = jnp.cumsum(sizes)
    firsts = ends - sizes
    places = jnp.arange(count, dtype=jnp.int32)
    inside = (places[None, :] >= firsts[:, None]) & (places[None, :] < ends[:, None])
    return jnp.sum(jnp.where(inside, firsts[:, None], 0), axis=0)


def rope_tables(positions):
    half = HD // 2
    freq = rope_base ** (-(jnp.arange(half, dtype=jnp.float32) * (2.0 / HD)))
    angle = freq[:, None] * positions.astype(jnp.float32)[None, :]
    cosine = jnp.concatenate([jnp.cos(angle), jnp.cos(angle)], axis=0)
    sine = jnp.concatenate([jnp.sin(angle), jnp.sin(angle)], axis=0)
    return (cosine, sine)


def rotate(values, cosine, sine):
    half = HD // 2
    turned = jnp.concatenate([-values[:, half:], values[:, :half]], axis=1)
    return values * cosine + turned * sine


def rotate_back(grads, cosine, sine):
    half = HD // 2
    lifted = grads * sine
    turned = jnp.concatenate([lifted[:, half:], -lifted[:, :half]], axis=1)
    return grads * cosine + turned


def contract_first(left, right):
    return lax.dot_general(
        left, right, (((0,), (0,)), ((), ())), preferred_element_type=jnp.float32
    )


def contract_last(left, right):
    return lax.dot_general(
        left, right, (((1,), (1,)), ((), ())), preferred_element_type=jnp.float32
    )


def feature_total(values):
    return lax.psum(jnp.sum(values, axis=0), "col")


def spread(values):
    return lax.all_gather(values, "col", axis=0, tiled=True)


def summed_rows(make_term, rows):
    return lax.psum_scatter(
        make_term(jnp.int32(0), lax.axis_size("col") * rows), "col", scatter_dimension=0, tiled=True
    )


def to_blocks(values):
    return lax.all_to_all(values, "col", split_axis=1, concat_axis=0, tiled=True)


def to_tokens(values):
    return lax.all_to_all(values, "col", split_axis=0, concat_axis=1, tiled=True)


def by_columns(weight, acts, start, count):
    return contract_first(weight, acts)


def by_rows(weight, grads, start, count):
    return jnp.dot(weight, grads, preferred_element_type=jnp.float32)


def by_rows_pair(first_weight, first_grads, second_weight, second_grads, start, count):
    return by_rows(first_weight, first_grads, start, count) + by_rows(
        second_weight, second_grads, start, count
    )


def norm_forward(residual, gain):
    totals = feature_total(residual * residual)
    scale = lax.rsqrt(totals / D + eps_norm)
    return (scale, (residual * scale * gain[:, None]).astype(jnp.bfloat16))


def norm_backward(d_normed, residual, scale, gain):
    weighted = d_normed * gain[:, None]
    inner = feature_total(weighted * residual)
    d_residual = weighted * scale - residual * (scale * scale * scale) * inner / D
    d_gain = jnp.sum(d_normed * residual * scale, axis=1)
    return (d_residual, d_gain)


def attend_scores(queries, keys, mask):
    scores = jnp.einsum(
        "kghq,khj->kgqj", queries, keys, preferred_element_type=jnp.float32
    ) * HD ** (-0.5)
    return jnp.where(mask[None, None], scores, neg_fill)


def per_device(
    hidden_states,
    out_grad,
    lengths,
    norm_gains,
    qkv_weight,
    qkv_bias,
    out_weight,
    gate_weight,
    up_weight,
    down_weight,
):
    feat_rows, tok_row = hidden_states.shape
    col_at = lax.axis_index("col")
    starts = row_starts(lengths[0], tok_row)
    positions = jnp.arange(tok_row, dtype=jnp.int32) - starts
    cosine, sine = rope_tables(positions)
    first = col_at * QB
    block_starts = lax.dynamic_slice_in_dim(starts, first, QB)
    cos_block = lax.dynamic_slice_in_dim(cosine, first, QB, 1)
    sin_block = lax.dynamic_slice_in_dim(sine, first, QB, 1)
    reach = QB + SEQ_MAX
    window = jnp.maximum(first - SEQ_MAX, 0)
    key_places = window + jnp.arange(reach, dtype=jnp.int32)
    query_places = first + jnp.arange(QB, dtype=jnp.int32)
    mask = (key_places[None, :] >= block_starts[:, None]) & (
        key_places[None, :] <= query_places[:, None]
    )
    group = HEADS // KV_HEADS
    rotary = HEADS + KV_HEADS
    query_rows = HEADS * HD
    kv_rows = KV_HEADS * HD
    gains = norm_gains.astype(jnp.float32)
    residual = hidden_states.astype(jnp.float32)
    saved = []
    for layer in range(LAYERS):
        w_qkv, b_qkv, w_out, w_gate, w_up, w_down = (
            lax.all_gather(qkv_weight[layer], "row", axis=0, tiled=True),
            lax.all_gather(qkv_bias[layer], "row", axis=1, tiled=True),
            lax.all_gather(out_weight[layer], "row", axis=1, tiled=True),
            lax.all_gather(gate_weight[layer], "row", axis=0, tiled=True),
            lax.all_gather(up_weight[layer], "row", axis=0, tiled=True),
            lax.all_gather(down_weight[layer], "row", axis=1, tiled=True),
        )
        scale_one, normed_one = norm_forward(residual, gains[layer, 0])
        full_one = spread(normed_one)
        raw = contract_first(w_qkv, full_one) + b_qkv.reshape(-1).astype(jnp.float32)[:, None]
        local_heads = raw.shape[0] // HD
        shaped = raw.reshape(local_heads, HD, tok_row)
        head_ids = col_at * local_heads + jnp.arange(local_heads)
        turned = jnp.where((head_ids < rotary)[:, None, None], rotate(shaped, cosine, sine), shaped)
        blocked = to_blocks(turned.reshape(raw.shape).astype(jnp.bfloat16))
        kv_full = lax.all_gather(blocked[query_rows:], "col", axis=1, tiled=True)
        kv_window = lax.dynamic_slice_in_dim(kv_full, window, reach, 1)
        queries = blocked[:query_rows].reshape(KV_HEADS, group, HD, QB)
        keys = kv_window[:kv_rows].reshape(KV_HEADS, HD, reach)
        values = kv_window[kv_rows:].reshape(KV_HEADS, HD, reach)
        masked = attend_scores(queries, keys, mask)
        row_top = jnp.max(masked, axis=-1, keepdims=True)
        lifted = jnp.exp(masked - row_top)
        row_mass = jnp.sum(lifted, axis=-1, keepdims=True)
        probs = lifted / row_mass
        log_mass = row_top + jnp.log(row_mass)
        mixed = (
            jnp.einsum(
                "kgqj,khj->kghq",
                probs.astype(jnp.bfloat16),
                values,
                preferred_element_type=jnp.float32,
            )
            .reshape(query_rows, QB)
            .astype(jnp.bfloat16)
        )
        carried = to_tokens(mixed)
        attention = summed_rows(partial(by_columns, w_out, carried), feat_rows)
        residual_mid = residual + attention
        scale_two, normed_two = norm_forward(residual_mid, gains[layer, 1])
        full_two = spread(normed_two)
        gate = contract_first(w_gate, full_two)
        up = contract_first(w_up, full_two)
        hidden = (gate * jax.nn.sigmoid(gate) * up).astype(jnp.bfloat16)
        feed = summed_rows(partial(by_columns, w_down, hidden), feat_rows)
        saved.append(
            (
                residual,
                scale_one,
                full_one,
                blocked,
                kv_window,
                log_mass,
                mixed,
                carried,
                residual_mid,
                scale_two,
                full_two,
                gate,
                up,
                hidden,
                (w_qkv, w_out, w_gate, w_up, w_down),
                local_heads,
            )
        )
        residual = residual_mid + feed
    out_states = residual.astype(jnp.bfloat16)
    grad = out_grad.astype(jnp.float32)
    layer_grads = [None] * LAYERS
    gain_terms = [None] * LAYERS
    for layer in reversed(range(LAYERS)):
        (
            residual_in,
            scale_one,
            full_one,
            blocked,
            kv_window,
            log_mass,
            mixed,
            carried,
            residual_mid,
            scale_two,
            full_two,
            gate,
            up,
            hidden,
            weights_full,
            local_heads,
        ) = saved[layer]
        w_qkv, w_out, w_gate, w_up, w_down = weights_full
        grad_full = spread(grad.astype(jnp.bfloat16))
        d_down = contract_last(hidden, grad_full)
        d_hidden = jnp.dot(w_down, grad_full, preferred_element_type=jnp.float32)
        squash = jax.nn.sigmoid(gate)
        d_gate = (d_hidden * up * squash * (1.0 + gate * (1.0 - squash))).astype(jnp.bfloat16)
        d_up = (d_hidden * gate * squash).astype(jnp.bfloat16)
        d_gate_w = contract_last(full_two, d_gate)
        d_up_w = contract_last(full_two, d_up)
        d_normed_two = summed_rows(partial(by_rows_pair, w_gate, d_gate, w_up, d_up), feat_rows)
        d_residual, d_gain_two = norm_backward(
            d_normed_two, residual_mid, scale_two, gains[layer, 1]
        )
        grad = grad + d_residual
        grad_full = spread(grad.astype(jnp.bfloat16))
        d_out_w = contract_last(carried, grad_full)
        d_mixed = to_blocks(
            jnp.dot(w_out, grad_full, preferred_element_type=jnp.float32).astype(jnp.bfloat16)
        )
        queries = blocked[:query_rows].reshape(KV_HEADS, group, HD, QB)
        keys = kv_window[:kv_rows].reshape(KV_HEADS, HD, reach)
        values = kv_window[kv_rows:].reshape(KV_HEADS, HD, reach)
        masked = attend_scores(queries, keys, mask)
        probs = jnp.exp(masked - log_mass)
        low_probs = probs.astype(jnp.bfloat16)
        d_heads_mix = d_mixed.reshape(KV_HEADS, group, HD, QB)
        d_probs = jnp.einsum(
            "kghq,khj->kgqj", d_heads_mix, values, preferred_element_type=jnp.float32
        )
        inner = jnp.sum(probs * d_probs, axis=-1, keepdims=True)
        d_scores = (probs * (d_probs - inner)).astype(jnp.bfloat16)
        d_queries = (
            jnp.einsum("kgqj,khj->kghq", d_scores, keys, preferred_element_type=jnp.float32)
            * HD ** (-0.5)
        ).reshape(query_rows, QB)
        d_keys = (
            jnp.einsum("kgqj,kghq->khj", d_scores, queries, preferred_element_type=jnp.float32)
            * HD ** (-0.5)
        ).reshape(kv_rows, reach)
        d_values = jnp.einsum(
            "kgqj,kghq->khj", low_probs, d_heads_mix, preferred_element_type=jnp.float32
        ).reshape(kv_rows, reach)
        d_window = jnp.concatenate([d_keys, d_values], axis=0)
        d_placed = lax.dynamic_update_slice_in_dim(
            jnp.zeros((2 * kv_rows, tok_row), jnp.float32), d_window, window, 1
        )
        d_kv = lax.psum_scatter(d_placed, "col", scatter_dimension=1, tiled=True)
        d_heads = jnp.concatenate([d_queries, d_kv], axis=0).reshape(HEADS + 2 * KV_HEADS, HD, QB)
        d_turned = jnp.concatenate(
            [rotate_back(d_heads[:rotary], cos_block, sin_block), d_heads[rotary:]], axis=0
        )
        d_raw = to_tokens(d_turned.reshape((HEADS + 2 * KV_HEADS) * HD, QB).astype(jnp.bfloat16))
        d_bias = jnp.sum(d_raw, axis=1, dtype=jnp.float32).reshape(local_heads, HD)
        d_qkv_w = contract_last(full_one, d_raw)
        d_normed_one = summed_rows(partial(by_rows, w_qkv, d_raw), feat_rows)
        d_residual, d_gain_one = norm_backward(
            d_normed_one, residual_in, scale_one, gains[layer, 0]
        )
        grad = grad + d_residual
        layer_grads[layer] = (
            lax.psum_scatter(d_qkv_w, "row", scatter_dimension=0, tiled=True),
            lax.psum_scatter(d_bias, "row", scatter_dimension=1, tiled=True),
            lax.psum_scatter(d_out_w, "row", scatter_dimension=1, tiled=True),
            lax.psum_scatter(d_gate_w, "row", scatter_dimension=0, tiled=True),
            lax.psum_scatter(d_up_w, "row", scatter_dimension=0, tiled=True),
            lax.psum_scatter(d_down, "row", scatter_dimension=1, tiled=True),
        )
        gain_terms[layer] = jnp.stack([d_gain_one, d_gain_two])
    gain_grads = lax.psum(jnp.stack(gain_terms), "row")
    stacked = [jnp.stack([entry[member] for entry in layer_grads]) for member in range(6)]
    return (
        out_states,
        grad,
        gain_grads,
        stacked[0],
        stacked[1],
        stacked[2],
        stacked[3],
        stacked[4],
        stacked[5],
    )


def solution(mesh):
    placed = (
        P("col", "row"),
        P("col", "row"),
        P("row", None),
        P(None, None, "col"),
        P(None, "row", "col"),
        P(None, "col", "row"),
        P(None, "col", "row"),
        P(None, "row", "col"),
        P(None, "row", "col"),
        P(None, "col", "row"),
    )
    return jax.shard_map(
        per_device,
        mesh=mesh,
        in_specs=placed,
        out_specs=(
            P("col", "row"),
            P("col", "row"),
            P(None, None, "col"),
            P(None, "row", "col"),
            P(None, "col", "row"),
            P(None, "col", "row"),
            P(None, "row", "col"),
            P(None, "row", "col"),
            P(None, "col", "row"),
        ),
        check_vma=False,
    )
```

profile of v0, /device:TPU:0, one launch (start us, length us, event | category | flops | bytes accessed | tf_op | source)
XLA Modules:
  0.0 2292.5 jit_solution(13109288929776706779)
XLA Ops:
  10.0 18.1 psum.63
  55.3 12.4 all-gather.29.cloned.1.call-done
  76.5 17.7 all_to_all.128
  95.2 22.6 all-gather.31.cloned.1.call-done
  153.3 66.9 %reduce-scatter.67.cloned.1.call-done = f32[192,1024]{1,0:T(8,128)} async-done(((f32[1536,1024]{1,0:T(8,128)}), f32[192,1024]{1,0:T(8,128)}) %reduce-scatter.67.cloned.1.call-update) | async-done | bytes 786448 | tf_op jit(solution)/shard_map/reduce_scatter | solution.py:70
  221.4 13.8 psum.64
  241.1 32.1 %all-gather.33.cloned.1.call-done = bf16[1536,1024]{1,0:T(8,128)(2,1)} async-done(((bf16[192,1024]{1,0:T(8,128)(2,1)}), bf16[1536,1024]{1,0:T(8,128)(2,1)}) %all-gather.33.cloned.1.call-update) | async-done | bytes 3145744 | tf_op jit(solution)/shard_map/all_gather | solution.py:66
  282.0 38.5 %all-gather.51.cloned.1.call-done = bf16[1,1536,1120]{1,2,0:T(8,128)(2,1)} async-done(((bf16[1,384,1120]{1,2,0:T(8,128)(2,1)}), bf16[1,1536,1120]{1,2,0:T(8,128)(2,1)}) %all-gather.51.cloned.1.call-update) | async-done | bytes 3440656 | tf_op jit(solution)/shard_map/all_gather | solution.py:159
  331.7 36.8 %all-gather.53.cloned.1.call-done = bf16[1,1120,1536]{2,1,0:T(8,128)(2,1)} async-done(((bf16[1,1120,384]{2,1,0:T(8,128)(2,1)}), bf16[1,1120,1536]{2,1,0:T(8,128)(2,1)}) %all-gather.53.cloned.1.call-update) | async-done | bytes 3440656 | tf_op jit(solution)/shard_map/all_gather | solution.py:160
  384.8 69.8 %reduce-scatter.69.cloned.1.call-done = f32[192,1024]{1,0:T(8,128)} async-done(((f32[1536,1024]{1,0:T(8,128)}), f32[192,1024]{1,0:T(8,128)}) %reduce-scatter.69.cloned.1.call-update) | async-done | bytes 786448 | tf_op jit(solution)/shard_map/reduce_scatter | solution.py:70
  455.9 13.7 psum.65
  492.0 15.5 all-gather.35.cloned.1.call-done
  516.2 17.8 all_to_all.129
  534.7 22.8 all-gather.37.cloned.1.call-done
  590.3 68.1 %reduce-scatter.71.cloned.1.call-done = f32[192,1024]{1,0:T(8,128)} async-done(((f32[1536,1024]{1,0:T(8,128)}), f32[192,1024]{1,0:T(8,128)}) %reduce-scatter.71.cloned.1.call-update) | async-done | bytes 786448 | tf_op jit(solution)/shard_map/reduce_scatter | solution.py:70
  659.6 13.7 psum.66
  676.8 27.9 %all-gather.57.cloned.1.call-done = bf16[1,1536,1120]{1,2,0:T(8,128)(2,1)} async-done(((bf16[1,384,1120]{1,2,0:T(8,128)(2,1)}), bf16[1,1536,1120]{1,2,0:T(8,128)(2,1)}) %all-gather.57.cloned.1.call-update) | async-done | bytes 3440656 | tf_op jit(solution)/shard_map/all_gather | solution.py:159
  704.7 40.1 %all-gather.39.cloned.1.call-done = bf16[1536,1024]{1,0:T(8,128)(2,1)} async-done(((bf16[192,1024]{1,0:T(8,128)(2,1)}), bf16[1536,1024]{1,0:T(8,128)(2,1)}) %all-gather.39.cloned.1.call-update) | async-done | bytes 3145744 | tf_op jit(solution)/shard_map/all_gather | solution.py:66
  753.6 38.1 %all-gather.55.cloned.1.call-done = bf16[1,1536,1120]{1,2,0:T(8,128)(2,1)} async-done(((bf16[1,384,1120]{1,2,0:T(8,128)(2,1)}), bf16[1,1536,1120]{1,2,0:T(8,128)(2,1)}) %all-gather.55.cloned.1.call-update) | async-done | bytes 3440656 | tf_op jit(solution)/shard_map/all_gather | solution.py:158
  800.5 38.9 %all-gather.59.cloned.1.call-done = bf16[1,1120,1536]{2,1,0:T(8,128)(2,1)} async-done(((bf16[1,1120,384]{2,1,0:T(8,128)(2,1)}), bf16[1,1120,1536]{2,1,0:T(8,128)(2,1)}) %all-gather.59.cloned.1.call-update) | async-done | bytes 3440656 | tf_op jit(solution)/shard_map/all_gather | solution.py:160
  839.4 39.7 %all-gather.41.cloned.1.call-done = bf16[1536,1024]{1,0:T(8,128)(2,1)} async-done(((bf16[192,1024]{1,0:T(8,128)(2,1)}), bf16[1536,1024]{1,0:T(8,128)(2,1)}) %all-gather.41.cloned.1.call-update) | async-done | bytes 3145744 | tf_op jit(solution)/shard_map/all_gather | solution.py:66
  879.1 12.5 fusion.14
  909.3 68.8 %reduce-scatter.75.cloned.1.call-done = f32[192,1024]{1,0:T(8,128)} async-done(((f32[1536,1024]{1,0:T(8,128)}), f32[192,1024]{1,0:T(8,128)}) %reduce-scatter.75.cloned.1.call-update) | async-done | bytes 786448 | tf_op jit(solution)/shard_map/reduce_scatter | solution.py:70
  980.0 13.6 psum.67
  995.8 36.7 %all-gather.43.cloned.1.call-done = bf16[1536,1024]{1,0:T(8,128)(2,1)} async-done(((bf16[192,1024]{1,0:T(8,128)(2,1)}), bf16[1536,1024]{1,0:T(8,128)(2,1)}) %all-gather.43.cloned.1.call-update) | async-done | bytes 3145744 | tf_op jit(solution)/shard_map/all_gather | solution.py:66
  1072.1 30.5 %reduce-scatter.43.cloned.1.call-done = f32[512,128]{1,0:T(8,128)} async-done(((f32[512,1024]{1,0:T(8,128)}), f32[512,128]{1,0:T(8,128)}) %reduce-scatter.43.cloned.1.call-update) | async-done | bytes 262160 | tf_op jit(solution)/shard_map/reduce_scatter | solution.py:290
  1106.0 17.7 all_to_all.130
  1150.8 52.5 %reduce-scatter.77.cloned.1.call-done = f32[192,1024]{1,0:T(8,128)} async-done(((f32[1536,1024]{1,0:T(8,128)}), f32[192,1024]{1,0:T(8,128)}) %reduce-scatter.77.cloned.1.call-update) | async-done | bytes 786448 | tf_op jit(solution)/shard_map/reduce_scatter | solution.py:70
  1205.2 14.7 psum.68
  1219.9 54.1 %reduce-scatter.73.cloned.1.call-done = f32[192,1024]{1,0:T(8,128)} async-done(((f32[1536,1024]{1,0:T(8,128)}), f32[192,1024]{1,0:T(8,128)}) %reduce-scatter.73.cloned.1.call-update) | async-done | bytes 786448 | tf_op jit(solution)/shard_map/reduce_scatter | solution.py:70
  1277.1 36.1 %all-gather.45.cloned.1.call-done = bf16[1536,1024]{1,0:T(8,128)(2,1)} async-done(((bf16[192,1024]{1,0:T(8,128)(2,1)}), bf16[1536,1024]{1,0:T(8,128)(2,1)}) %all-gather.45.cloned.1.call-update) | async-done | bytes 3145744 | tf_op jit(solution)/shard_map/all_gather | solution.py:66
  1341.7 68.6 %reduce-scatter.79.cloned.1.call-done = f32[192,1024]{1,0:T(8,128)} async-done(((f32[1536,1024]{1,0:T(8,128)}), f32[192,1024]{1,0:T(8,128)}) %reduce-scatter.79.cloned.1.call-update) | async-done | bytes 786448 | tf_op jit(solution)/shard_map/reduce_scatter | solution.py:70
  1411.6 13.7 psum.69
  1427.8 36.7 %all-gather.47.cloned.1.call-done = bf16[1536,1024]{1,0:T(8,128)(2,1)} async-done(((bf16[192,1024]{1,0:T(8,128)(2,1)}), bf16[1536,1024]{1,0:T(8,128)(2,1)}) %all-gather.47.cloned.1.call-update) | async-done | bytes 3145744 | tf_op jit(solution)/shard_map/all_gather | solution.py:66
  1569.3 17.9 all_to_all.131
  1607.8 29.6 %reduce-scatter.65.cloned.1.call-done = f32[1120,384]{1,0:T(8,128)} async-done(((f32[1120,1536]{1,0:T(8,128)}), f32[1120,384]{1,0:T(8,128)}) %reduce-scatter.65.cloned.1.call-update) | async-done | bytes 1720336 | tf_op jit(solution)/shard_map/reduce_scatter | solution.py:309
  1637.4 77.8 %reduce-scatter.63.cloned.1.call-done = f32[1120,384]{1,0:T(8,128)} async-done(((f32[1120,1536]{1,0:T(8,128)}), f32[1120,384]{1,0:T(8,128)}) %reduce-scatter.63.cloned.1.call-update) | async-done | bytes 1720336 | tf_op jit(solution)/shard_map/reduce_scatter | solution.py:309
  1719.2 73.9 %reduce-scatter.61.cloned.1.call-done = f32[384,1120]{0,1:T(8,128)} async-done(((f32[1536,1120]{0,1:T(8,128)}), f32[384,1120]{0,1:T(8,128)}) %reduce-scatter.61.cloned.1.call-update) | async-done | bytes 1720336 | tf_op jit(solution)/shard_map/reduce_scatter | solution.py:308
  1793.1 77.8 %reduce-scatter.59.cloned.1.call-done = f32[384,1120]{0,1:T(8,128)} async-done(((f32[1536,1120]{0,1:T(8,128)}), f32[384,1120]{0,1:T(8,128)}) %reduce-scatter.59.cloned.1.call-update) | async-done | bytes 1720336 | tf_op jit(solution)/shard_map/reduce_scatter | solution.py:308
  1874.9 73.9 %reduce-scatter.57.cloned.1.call-done = f32[384,1120]{0,1:T(8,128)} async-done(((f32[1536,1120]{0,1:T(8,128)}), f32[384,1120]{0,1:T(8,128)}) %reduce-scatter.57.cloned.1.call-update) | async-done | bytes 1720336 | tf_op jit(solution)/shard_map/reduce_scatter | solution.py:307
  1948.7 77.8 %reduce-scatter.55.cloned.1.call-done = f32[384,1120]{0,1:T(8,128)} async-done(((f32[1536,1120]{0,1:T(8,128)}), f32[384,1120]{0,1:T(8,128)}) %reduce-scatter.55.cloned.1.call-update) | async-done | bytes 1720336 | tf_op jit(solution)/shard_map/reduce_scatter | solution.py:307
  2030.5 27.6 %reduce-scatter.53.cloned.1.call-done = f32[192,384]{1,0:T(8,128)} async-done(((f32[192,1536]{1,0:T(8,128)}), f32[192,384]{1,0:T(8,128)}) %reduce-scatter.53.cloned.1.call-update) | async-done | bytes 294928 | tf_op jit(solution)/shard_map/reduce_scatter | solution.py:306
  2058.2 31.5 %reduce-scatter.51.cloned.1.call-done = f32[192,384]{1,0:T(8,128)} async-done(((f32[192,1536]{1,0:T(8,128)}), f32[192,384]{1,0:T(8,128)}) %reduce-scatter.51.cloned.1.call-update) | async-done | bytes 294928 | tf_op jit(solution)/shard_map/reduce_scatter | solution.py:306
  2091.6 24.9 %reduce-scatter.83.cloned.1.call-done = f32[32,2]{1,0:T(8,128)} async-done(((f32[128,2]{1,0:T(8,128)}), f32[32,2]{1,0:T(8,128)}) %reduce-scatter.83.cloned.1.call-update) | async-done | bytes 272
  2117.9 32.8 %reduce-scatter.49.cloned.1.call-done = f32[384,256]{1,0:T(8,128)} async-done(((f32[1536,256]{1,0:T(8,128)}), f32[384,256]{1,0:T(8,128)}) %reduce-scatter.49.cloned.1.call-update) | async-done | bytes 393232 | tf_op jit(solution)/shard_map/reduce_scatter | solution.py:304
  2150.7 34.2 %reduce-scatter.47.cloned.1.call-done = f32[384,256]{1,0:T(8,128)} async-done(((f32[1536,256]{1,0:T(8,128)}), f32[384,256]{1,0:T(8,128)}) %reduce-scatter.47.cloned.1.call-update) | async-done | bytes 393232 | tf_op jit(solution)/shard_map/reduce_scatter | solution.py:304
  2186.9 69.9 %reduce-scatter.81.cloned.1.call-done = f32[192,1024]{1,0:T(8,128)} async-done(((f32[1536,1024]{1,0:T(8,128)}), f32[192,1024]{1,0:T(8,128)}) %reduce-scatter.81.cloned.1.call-update) | async-done | bytes 786448 | tf_op jit(solution)/shard_map/reduce_scatter | solution.py:70
  2268.6 13.6 psum.70
  (410 shorter events, 490.3 us)
Async XLA Ops:
  8.0 59.7 %all-gather.29.cloned.1.call-start = ((), (), s32[]{:S(2)}) async-start(), calls=%async_computation.30 | async-start | bytes 3538944 | tf_op jit(solution)/shard_map/all_gather | solution.py:66
  8.8 461.3 %copy-start.67 = (f32[1,1,192]{2,1,0:T(1,128)}, f32[1,1,192]{2,1,0:T(1,128)S(1)}, u32[]{:S(2)}) copy-start(f32[1,1,192]{2,1,0:T(1,128)S(1)} %get-tuple-element.93) | copy-start | bytes 2308
  8.9 984.8 %copy-start.60 = (f32[1,1,192]{2,1,0:T(1,128)}, f32[1,1,192]{2,1,0:T(1,128)S(1)}, u32[]{:S(2)}) copy-start(f32[1,1,192]{2,1,0:T(1,128)S(1)} %get-tuple-element.92) | copy-start | bytes 2308
  31.1 86.7 %all-gather.31.cloned.1.call-start = ((), (), s32[]{:S(2)}) async-start(), calls=%async_computation.31 | async-start | bytes 1179648 | tf_op jit(solution)/shard_map/all_gather | solution.py:170
  123.6 16.3 all-to-all-start.1
  127.2 92.9 %reduce-scatter.67.cloned.1.call-start = ((), (), s32[]{:S(2)}) async-start(), calls=%async_computation.58 | async-start | bytes 7077888 | tf_op jit(solution)/shard_map/reduce_scatter | solution.py:70
  150.3 90.8 %all-gather.49.cloned.1.call-start = ((), (), s32[]{:S(2)}) async-start(), calls=%async_computation.52 | async-start | bytes 4300800 | tf_op jit(solution)/shard_map/all_gather | solution.py:158
  153.2 120.0 %all-gather.33.cloned.1.call-start = ((), (), s32[]{:S(2)}) async-start(), calls=%async_computation.32 | async-start | bytes 3538944 | tf_op jit(solution)/shard_map/all_gather | solution.py:66
  221.4 233.2 %copy-start.4 = (f32[192,1024]{1,0:T(8,128)}, f32[192,1024]{1,0:T(8,128)S(1)}, u32[]{:S(2)}) copy-start(f32[192,1024]{1,0:T(8,128)S(1)} %get-tuple-element.53) | copy-start | bytes 2359300
  236.8 83.8 %all-gather.51.cloned.1.call-start = ((), (), s32[]{:S(2)}) async-start(), calls=%async_computation.53 | async-start | bytes 4300800 | tf_op jit(solution)/shard_map/all_gather | solution.py:159
  239.6 128.8 %all-gather.53.cloned.1.call-start = ((), (), s32[]{:S(2)}) async-start(), calls=%async_computation.54 | async-start | bytes 4300800 | tf_op jit(solution)/shard_map/all_gather | solution.py:160
  241.1 213.5 %reduce-scatter.69.cloned.1.call-start = ((), (), s32[]{:S(2)}) async-start(), calls=%async_computation.59 | async-start | bytes 7077888 | tf_op jit(solution)/shard_map/reduce_scatter | solution.py:70
  384.7 122.8 %all-gather.35.cloned.1.call-start = ((), (), s32[]{:S(2)}) async-start(), calls=%async_computation.33 | async-start | bytes 3538944 | tf_op jit(solution)/shard_map/all_gather | solution.py:66
  471.0 86.4 %all-gather.37.cloned.1.call-start = ((), (), s32[]{:S(2)}) async-start(), calls=%async_computation.34 | async-start | bytes 1179648 | tf_op jit(solution)/shard_map/all_gather | solution.py:170
  563.2 16.0 all-to-all-start.3
  566.7 91.7 %reduce-scatter.71.cloned.1.call-start = ((), (), s32[]{:S(2)}) async-start(), calls=%async_computation.60 | async-start | bytes 7077888 | tf_op jit(solution)/shard_map/reduce_scatter | solution.py:70
  589.6 115.0 %all-gather.57.cloned.1.call-start = ((), (), s32[]{:S(2)}) async-start(), calls=%async_computation.56 | async-start | bytes 4300800 | tf_op jit(solution)/shard_map/all_gather | solution.py:159
  590.2 154.6 %all-gather.39.cloned.1.call-start = ((), (), s32[]{:S(2)}) async-start(), calls=%async_computation.35 | async-start | bytes 3538944 | tf_op jit(solution)/shard_map/all_gather | solution.py:66
  673.4 320.3 %copy-start.54 = (f32[1024]{0:T(1024)}, f32[1024]{0:T(1024)S(1)}, u32[]{:S(2)}) copy-start(f32[1024]{0:T(1024)S(1)} %get-tuple-element.90) | copy-start | bytes 12292
  674.3 117.4 %all-gather.55.cloned.1.call-start = ((), (), s32[]{:S(2)}) async-start(), calls=%async_computation.55 | async-start | bytes 4300800 | tf_op jit(solution)/shard_map/all_gather | solution.py:158
  675.0 164.4 %all-gather.59.cloned.1.call-start = ((), (), s32[]{:S(2)}) async-start(), calls=%async_computation.57 | async-start | bytes 4300800 | tf_op jit(solution)/shard_map/all_gather | solution.py:160
  675.6 203.6 %all-gather.41.cloned.1.call-start = ((), (), s32[]{:S(2)}) async-start(), calls=%async_computation.36 | async-start | bytes 3538944 | tf_op jit(solution)/shard_map/all_gather | solution.py:66
  676.3 301.8 %reduce-scatter.75.cloned.1.call-start = ((), (), s32[]{:S(2)}) async-start(), calls=%async_computation.62 | async-start | bytes 7077888 | tf_op jit(solution)/shard_map/reduce_scatter | solution.py:70
  909.3 123.3 %all-gather.43.cloned.1.call-start = ((), (), s32[]{:S(2)}) async-start(), calls=%async_computation.37 | async-start | bytes 3538944 | tf_op jit(solution)/shard_map/all_gather | solution.py:66
  1036.1 15.9 all-to-all-start.4
  1039.5 63.1 %reduce-scatter.43.cloned.1.call-start = ((), (), s32[]{:S(2)}) async-start(), calls=%async_computation.38 | async-start | bytes 2359296 | tf_op jit(solution)/shard_map/reduce_scatter | solution.py:290
  1067.9 135.4 %reduce-scatter.77.cloned.1.call-start = ((), (), s32[]{:S(2)}) async-start(), calls=%async_computation.63 | async-start | bytes 7077888 | tf_op jit(solution)/shard_map/reduce_scatter | solution.py:70
  1134.4 139.6 %reduce-scatter.73.cloned.1.call-start = ((), (), s32[]{:S(2)}) async-start(), calls=%async_computation.61 | async-start | bytes 7077888 | tf_op jit(solution)/shard_map/reduce_scatter | solution.py:70
  1150.7 162.6 %all-gather.45.cloned.1.call-start = ((), (), s32[]{:S(2)}) async-start(), calls=%async_computation.39 | async-start | bytes 3538944 | tf_op jit(solution)/shard_map/all_gather | solution.py:66
  1276.7 133.6 %reduce-scatter.79.cloned.1.call-start = ((), (), s32[]{:S(2)}) async-start(), calls=%async_computation.64 | async-start | bytes 7077888 | tf_op jit(solution)/shard_map/reduce_scatter | solution.py:70
  1341.6 122.8 %all-gather.47.cloned.1.call-start = ((), (), s32[]{:S(2)}) async-start(), calls=%async_computation.40 | async-start | bytes 3538944 | tf_op jit(solution)/shard_map/all_gather | solution.py:66
  1468.0 16.1 all-to-all-start.6
  1471.6 95.5 %reduce-scatter.45.cloned.1.call-start = ((), (), s32[]{:S(2)}) async-start(), calls=%async_computation.41 | async-start | bytes 2359296 | tf_op jit(solution)/shard_map/reduce_scatter | solution.py:290
  1498.6 108.4 %reduce-scatter.85.cloned.1.call-start = ((), (), s32[]{:S(2)}) async-start(), calls=%async_computation.67 | async-start | bytes 81920
  1500.6 136.8 %reduce-scatter.65.cloned.1.call-start = ((), (), s32[]{:S(2)}) async-start(), calls=%async_computation.51 | async-start | bytes 8601600 | tf_op jit(solution)/shard_map/reduce_scatter | solution.py:309
  1509.8 205.4 %reduce-scatter.63.cloned.1.call-start = ((), (), s32[]{:S(2)}) async-start(), calls=%async_computation.50 | async-start | bytes 8601600 | tf_op jit(solution)/shard_map/reduce_scatter | solution.py:309
  1519.1 273.9 %reduce-scatter.61.cloned.1.call-start = ((), (), s32[]{:S(2)}) async-start(), calls=%async_computation.49 | async-start | bytes 8601600 | tf_op jit(solution)/shard_map/reduce_scatter | solution.py:308
  1528.7 342.1 %reduce-scatter.59.cloned.1.call-start = ((), (), s32[]{:S(2)}) async-start(), calls=%async_computation.48 | async-start | bytes 8601600 | tf_op jit(solution)/shard_map/reduce_scatter | solution.py:308
  1538.0 410.7 %reduce-scatter.57.cloned.1.call-start = ((), (), s32[]{:S(2)}) async-start(), calls=%async_computation.47 | async-start | bytes 8601600 | tf_op jit(solution)/shard_map/reduce_scatter | solution.py:307
  1547.3 479.2 %reduce-scatter.55.cloned.1.call-start = ((), (), s32[]{:S(2)}) async-start(), calls=%async_computation.46 | async-start | bytes 8601600 | tf_op jit(solution)/shard_map/reduce_scatter | solution.py:307
  1556.9 501.3 %reduce-scatter.53.cloned.1.call-start = ((), (), s32[]{:S(2)}) async-start(), calls=%async_computation.45 | async-start | bytes 1474560 | tf_op jit(solution)/shard_map/reduce_scatter | solution.py:306
  1562.0 527.7 %reduce-scatter.51.cloned.1.call-start = ((), (), s32[]{:S(2)}) async-start(), calls=%async_computation.44 | async-start | bytes 1474560 | tf_op jit(solution)/shard_map/reduce_scatter | solution.py:306
  1566.2 550.3 %reduce-scatter.83.cloned.1.call-start = ((), (), s32[]{:S(2)}) async-start(), calls=%async_computation.66 | async-start | bytes 81920
  1588.1 562.6 %reduce-scatter.49.cloned.1.call-start = ((), (), s32[]{:S(2)}) async-start(), calls=%async_computation.43 | async-start | bytes 1966080 | tf_op jit(solution)/shard_map/reduce_scatter | solution.py:304
  1592.2 592.6 %reduce-scatter.47.cloned.1.call-start = ((), (), s32[]{:S(2)}) async-start(), calls=%async_computation.42 | async-start | bytes 1966080 | tf_op jit(solution)/shard_map/reduce_scatter | solution.py:304
  1596.6 660.2 %reduce-scatter.81.cloned.1.call-start = ((), (), s32[]{:S(2)}) async-start(), calls=%async_computation.65 | async-start | bytes 7077888 | tf_op jit(solution)/shard_map/reduce_scatter | solution.py:70
  2030.5 251.7 %copy-start.29 = (f32[192,1024]{1,0:T(8,128)S(1)}, f32[192,1024]{1,0:T(8,128)}, u32[]{:S(2)}) copy-start(f32[192,1024]{1,0:T(8,128)} %get-tuple-element.45) | copy-start | bytes 2359300
  2030.5 251.7 %copy-start.63 = (f32[1024]{0:T(1024)S(1)}, f32[1024]{0:T(1024)}, u32[]{:S(2)}) copy-start(f32[1024]{0:T(1024)} %get-tuple-element.84) | copy-start | bytes 12292
  (73 other events, 2595.3 us)
Sparse Core Ops, SparseCore 0:
  31.3 36.4 all-gather.28
  95.1 22.7 all-gather.30
  150.4 69.6 reduce-scatter.66
  384.9 69.7 reduce-scatter.68
  909.4 68.6 reduce-scatter.74
  996.0 36.5 all-gather.42
  1068.0 34.5 reduce-scatter.42
  1134.5 68.7 reduce-scatter.76
  1205.6 68.3 reduce-scatter.72
  1427.9 36.5 all-gather.46
  1498.7 34.5 reduce-scatter.44
  1536.4 22.9 reduce-scatter.84
  1562.5 74.9 reduce-scatter.64
  1640.3 74.9 reduce-scatter.62
  1718.1 74.9 reduce-scatter.60
  1795.9 74.9 reduce-scatter.58
  1873.7 74.9 reduce-scatter.56
  1951.6 74.9 reduce-scatter.54
  2029.4 28.6 reduce-scatter.52
  2060.9 28.6 reduce-scatter.50
  2092.4 24.0 reduce-scatter.82
  2119.5 31.1 reduce-scatter.48
  2153.7 31.1 reduce-scatter.46
  2187.0 69.7 reduce-scatter.80
Sparse Core Ops, SparseCore 1:
  153.3 46.0 all-gather.48
  236.8 36.3 all-gather.32
  275.5 45.0 all-gather.50
  322.4 46.0 all-gather.52
  471.1 36.3 all-gather.34
  534.7 22.7 all-gather.36
  589.7 68.6 reduce-scatter.70
  660.1 44.5 all-gather.56
  706.7 38.0 all-gather.38
  746.6 45.0 all-gather.54
  793.4 46.0 all-gather.58
  841.1 38.0 all-gather.40
  1276.8 36.5 all-gather.44
  1341.7 68.6 reduce-scatter.78
where the time goes:
time: 2300 us; the launch traced here: 2290 us
  waiting for transfers between devices  1610 us (70%)
  blocking collectives  260 us (11%)
  matrix products  220 us (10%)
  local copies, waits for them, and re-layouts  99 us (4%)
  other arithmetic  63.8 us (3%)
    reduce_scatter x8, waiting for transfers between devices, summed_rows(): lax.psum_scatter(make_term(jnp.int32(0), lax.axis_size('col') * rows), 'c...  519 us
    all_gather x8, waiting for transfers between devices, spread(): return lax.all_gather(values, 'col', axis=0, tiled=True)  249 us
    reduce_scatter x2, waiting for transfers between devices, per_device(): lax.psum_scatter(d_up_w, 'row', scatter_dimension=0, tiled=True)  152 us
    reduce_scatter x2, waiting for transfers between devices, per_device(): lax.psum_scatter(d_gate_w, 'row', scatter_dimension=0, tiled=True)  152 us
    psum x8, blocking collectives, feature_total(): return lax.psum(jnp.sum(values, axis=0), 'col')  115 us
    reduce_scatter x2, waiting for transfers between devices, per_device(): lax.psum_scatter(d_down, 'row', scatter_dimension=1, tiled=True)  107 us
    all_gather x2, waiting for transfers between devices, per_device(): lax.all_gather(down_weight[layer], 'row', axis=1, tiled=True)  75.7 us
    dot_general x10, matrix products, contract_last(): lax.dot_general(left, right, (((1,), (1,)), ((), ())), preferred_element_...  71.6 us
  transfers between devices with their start and end apart: 42, of which 38 were waited for; matrix products, arithmetic and copies ran while one was open for 8% of the time, Pallas kernels for 0%

commit v1 on v0

--- a/solution.py
+++ b/solution.py
@@ -16,6 +16,11 @@
 neg_fill = -1e30
 
 
+def swapped_in(block, axis, dim):
+    sent = jnp.stack([block] * lax.axis_size(axis))
+    return jnp.concatenate(lax.all_to_all(sent, axis, 0, 0), axis=dim)
+
+
 def row_starts(sizes, count):
     ends = jnp.cumsum(sizes)
     firsts = ends - sizes
@@ -63,7 +68,7 @@
 
 
 def spread(values):
-    return lax.all_gather(values, "col", axis=0, tiled=True)
+    return swapped_in(values, "col", 0)
 
 
 def summed_rows(make_term, rows):

time: 2300 us -> 2440 us (1.061)
  blocking collectives: 260 us -> 482 us
  waiting for transfers between devices: 1610 us -> 1470 us
  local copies, waits for them, and re-layouts: 99 us -> 143 us
    reduce_scatter x8 -> x0, waiting for transfers between devices: 519 us -> none  [summed_rows(): lax.psum_scatter(make_term(jnp.int32(0), lax.axis_size('col') * rows), 'c...]
    unnamed x40, waiting for transfers between devices: 28 us -> 542 us
    all_to_all x0 -> x5, waiting for transfers between devices: none -> 260 us  [swapped_in(): return jnp.concatenate(lax.all_to_all(sent, axis, 0, 0), axis=dim)]
    all_gather x8 -> x0, waiting for transfers between devices: 249 us -> none  [spread(): return lax.all_gather(values, 'col', axis=0, tiled=True)]
    all_to_all x0 -> x3, blocking collectives: none -> 223 us  [swapped_in(): return jnp.concatenate(lax.all_to_all(sent, axis, 0, 0), axis=dim)]
    all_gather x2, waiting for transfers between devices: 66.4 us -> 0.03 us  [per_device(): lax.all_gather(up_weight[layer], 'row', axis=0, tiled=True)]
    all_gather x2, waiting for transfers between devices: 75.7 us -> 30.9 us  [per_device(): lax.all_gather(down_weight[layer], 'row', axis=1, tiled=True)]
    all_gather x2, waiting for transfers between devices: 38.1 us -> 0.03 us  [per_device(): lax.all_gather(gate_weight[layer], 'row', axis=0, tiled=True)]
  transfers between devices with their start and end apart: 42 -> 39, of which waited for: 38 -> 32; matrix products, arithmetic and copies ran while one was open for 8% -> 8% of each run, Pallas kernels for 0% -> 0%
where the time goes in v1:
time: 2440 us; the launch traced here: 2430 us
  waiting for transfers between devices  1470 us (60%)
  blocking collectives  482 us (20%)
  matrix products  217 us (9%)
  local copies, waits for them, and re-layouts  143 us (6%)
  other arithmetic  62.8 us (3%)
  starting transfers between devices  39.5 us (2%)
    unnamed x40, waiting for transfers between devices  542 us
    all_to_all x5, waiting for transfers between devices, swapped_in(): return jnp.concatenate(lax.all_to_all(sent, axis, 0, 0), axis=dim)  260 us
    all_to_all x3, blocking collectives, swapped_in(): return jnp.concatenate(lax.all_to_all(sent, axis, 0, 0), axis=dim)  223 us
    reduce_scatter x2, waiting for transfers between devices, per_device(): lax.psum_scatter(d_up_w, 'row', scatter_dimension=0, tiled=True)  152 us
    reduce_scatter x2, waiting for transfers between devices, per_device(): lax.psum_scatter(d_gate_w, 'row', scatter_dimension=0, tiled=True)  152 us
    psum x8, blocking collectives, feature_total(): return lax.psum(jnp.sum(values, axis=0), 'col')  114 us
    reduce_scatter x2, waiting for transfers between devices, per_device(): lax.psum_scatter(d_down, 'row', scatter_dimension=1, tiled=True)  107 us
    unnamed x190, local copies, waits for them, and re-layouts  84.6 us
  transfers between devices with their start and end apart: 39, of which 32 were waited for; matrix products, arithmetic and copies ran while one was open for 8% of the time, Pallas kernels for 0%

profile of v1, /device:TPU:0, one launch (start us, length us, event | category | flops | bytes accessed | tf_op | source)
XLA Modules:
  0.0 2429.7 jit_solution(7483413580730255076)
XLA Ops:
  9.4 18.1 psum.63
  59.8 48.2 %all-to-all-done = bf16[8,192,1024]{2,1,0:T(8,128)(2,1)} async-done(((bf16[8,192,1024]{2,1,0:T(8,128)(2,1)}), bf16[8,192,1024]{2,1,0:T(8,128)(2,1)}, u32[]{:S(2)}, u32[]{:S(2)}) %all-to-all-start) | async-done | bytes 3145760 | tf_op jit(solution)/shard_map/all_to_all | solution.py:21
  116.1 17.7 all_to_all.168
  134.8 22.7 all-gather.21.cloned.1.call-done
  168.5 11.5 all-gather.2
  196.2 64.0 %reduce-scatter.67.cloned.1.call-done = f32[192,1024]{1,0:T(8,128)} async-done(((f32[1536,1024]{1,0:T(8,128)}), f32[192,1024]{1,0:T(8,128)}) %reduce-scatter.67.cloned.1.call-update) | async-done | bytes 786448
  264.1 13.7 psum.64
  288.9 68.5 %all-to-all-done.3 = bf16[8,192,1024]{2,1,0:T(8,128)(2,1)} async-done(((bf16[8,192,1024]{2,1,0:T(8,128)(2,1)}), bf16[8,192,1024]{2,1,0:T(8,128)(2,1)}, u32[]{:S(2)}, u32[]{:S(2)}) %all-to-all-start.3) | async-done | bytes 3145760 | tf_op jit(solution)/shard_map/all_to_all | solution.py:21
  393.6 68.9 %reduce-scatter.69.cloned.1.call-done = f32[192,1024]{1,0:T(8,128)} async-done(((f32[1536,1024]{1,0:T(8,128)}), f32[192,1024]{1,0:T(8,128)}) %reduce-scatter.69.cloned.1.call-update) | async-done | bytes 786448
  466.4 13.7 psum.65
  496.9 11.7 all-gather.6
  508.6 51.2 %all-to-all-done.4 = bf16[8,192,1024]{2,1,0:T(8,128)(2,1)} async-done(((bf16[8,192,1024]{2,1,0:T(8,128)(2,1)}), bf16[8,192,1024]{2,1,0:T(8,128)(2,1)}, u32[]{:S(2)}, u32[]{:S(2)}) %all-to-all-start.4) | async-done | bytes 3145760 | tf_op jit(solution)/shard_map/all_to_all | solution.py:21
  568.4 17.7 all_to_all.169
  586.9 23.0 all-gather.23.cloned.1.call-done
  619.3 11.5 all-gather.8
  642.9 68.2 %reduce-scatter.71.cloned.1.call-done = f32[192,1024]{1,0:T(8,128)} async-done(((f32[1536,1024]{1,0:T(8,128)}), f32[192,1024]{1,0:T(8,128)}) %reduce-scatter.71.cloned.1.call-update) | async-done | bytes 786448
  712.7 13.7 psum.66
  734.2 70.8 %all-to-all-done.7 = bf16[8,192,1024]{2,1,0:T(8,128)(2,1)} async-done(((bf16[8,192,1024]{2,1,0:T(8,128)(2,1)}), bf16[8,192,1024]{2,1,0:T(8,128)(2,1)}, u32[]{:S(2)}, u32[]{:S(2)}) %all-to-all-start.7) | async-done | bytes 3145760 | tf_op jit(solution)/shard_map/all_to_all | solution.py:21
  830.7 30.9 %all-gather.35.cloned.1.call-done = bf16[1,1120,1536]{2,1,0:T(8,128)(2,1)} async-done(((bf16[1,1120,384]{2,1,0:T(8,128)(2,1)}), bf16[1,1120,1536]{2,1,0:T(8,128)(2,1)}) %all-gather.35.cloned.1.call-update) | async-done | bytes 3440656 | tf_op jit(solution)/shard_map/all_gather | solution.py:165
  861.7 21.4 all-to-all-done.8
  883.0 12.5 fusion.14
  930.5 51.6 %reduce-scatter.75.cloned.1.call-done = f32[192,1024]{1,0:T(8,128)} async-done(((f32[1536,1024]{1,0:T(8,128)}), f32[192,1024]{1,0:T(8,128)}) %reduce-scatter.75.cloned.1.call-update) | async-done | bytes 786448
  984.4 14.1 psum.67
  998.5 54.2 %reduce-scatter.73.cloned.1.call-done = f32[192,1024]{1,0:T(8,128)} async-done(((f32[1536,1024]{1,0:T(8,128)}), f32[192,1024]{1,0:T(8,128)}) %reduce-scatter.73.cloned.1.call-update) | async-done | bytes 786448
  1058.8 74.1 %all_to_all.170 = bf16[8,192,1024]{2,1,0:T(8,128)(2,1)S(1)} all-to-all(bf16[8,192,1024]{2,1,0:T(8,128)(2,1)S(1)} %stack.75), channel_id=1, replica_groups=mesh['row'=4,'col'=8] {'col'}, dimensions={0} | all-to-all | bytes 6291456 | tf_op jit(solution)/shard_map/all_to_all | solution.py:21
  1172.4 30.2 %reduce-scatter.43.cloned.1.call-done = f32[512,128]{1,0:T(8,128)} async-done(((f32[512,1024]{1,0:T(8,128)}), f32[512,128]{1,0:T(8,128)}) %reduce-scatter.43.cloned.1.call-update) | async-done | bytes 262160 | tf_op jit(solution)/shard_map/reduce_scatter | solution.py:295
  1206.0 18.4 all_to_all.171
  1238.2 68.5 %reduce-scatter.77.cloned.1.call-done = f32[192,1024]{1,0:T(8,128)} async-done(((f32[1536,1024]{1,0:T(8,128)}), f32[192,1024]{1,0:T(8,128)}) %reduce-scatter.77.cloned.1.call-update) | async-done | bytes 786448
  1311.7 13.7 psum.68
  1330.5 74.5 %all_to_all.172 = bf16[8,192,1024]{2,1,0:T(8,128)(2,1)S(1)} all-to-all(bf16[8,192,1024]{2,1,0:T(8,128)(2,1)S(1)} %stack.76), channel_id=1, replica_groups=mesh['row'=4,'col'=8] {'col'}, dimensions={0} | all-to-all | bytes 6291456 | tf_op jit(solution)/shard_map/all_to_all | solution.py:21
  1431.3 68.8 %reduce-scatter.79.cloned.1.call-done = f32[192,1024]{1,0:T(8,128)} async-done(((f32[1536,1024]{1,0:T(8,128)}), f32[192,1024]{1,0:T(8,128)}) %reduce-scatter.79.cloned.1.call-update) | async-done | bytes 786448
  1505.0 13.7 psum.69
  1523.8 74.1 %all_to_all.173 = bf16[8,192,1024]{2,1,0:T(8,128)(2,1)S(1)} all-to-all(bf16[8,192,1024]{2,1,0:T(8,128)(2,1)S(1)} %stack.77), channel_id=1, replica_groups=mesh['row'=4,'col'=8] {'col'}, dimensions={0} | all-to-all | bytes 6291456 | tf_op jit(solution)/shard_map/all_to_all | solution.py:21
  1605.6 11.5 all-to-all-done.14
  1703.5 17.7 all_to_all.174
  1744.3 28.9 %reduce-scatter.65.cloned.1.call-done = f32[1120,384]{1,0:T(8,128)} async-done(((f32[1120,1536]{1,0:T(8,128)}), f32[1120,384]{1,0:T(8,128)}) %reduce-scatter.65.cloned.1.call-update) | async-done | bytes 1720336 | tf_op jit(solution)/shard_map/reduce_scatter | solution.py:314
  1773.1 77.8 %reduce-scatter.63.cloned.1.call-done = f32[1120,384]{1,0:T(8,128)} async-done(((f32[1120,1536]{1,0:T(8,128)}), f32[1120,384]{1,0:T(8,128)}) %reduce-scatter.63.cloned.1.call-update) | async-done | bytes 1720336 | tf_op jit(solution)/shard_map/reduce_scatter | solution.py:314
  1854.9 73.9 %reduce-scatter.61.cloned.1.call-done = f32[384,1120]{0,1:T(8,128)} async-done(((f32[1536,1120]{0,1:T(8,128)}), f32[384,1120]{0,1:T(8,128)}) %reduce-scatter.61.cloned.1.call-update) | async-done | bytes 1720336 | tf_op jit(solution)/shard_map/reduce_scatter | solution.py:313
  1928.8 77.8 %reduce-scatter.59.cloned.1.call-done = f32[384,1120]{0,1:T(8,128)} async-done(((f32[1536,1120]{0,1:T(8,128)}), f32[384,1120]{0,1:T(8,128)}) %reduce-scatter.59.cloned.1.call-update) | async-done | bytes 1720336 | tf_op jit(solution)/shard_map/reduce_scatter | solution.py:313
  2010.6 73.9 %reduce-scatter.57.cloned.1.call-done = f32[384,1120]{0,1:T(8,128)} async-done(((f32[1536,1120]{0,1:T(8,128)}), f32[384,1120]{0,1:T(8,128)}) %reduce-scatter.57.cloned.1.call-update) | async-done | bytes 1720336 | tf_op jit(solution)/shard_map/reduce_scatter | solution.py:312
  2084.4 77.8 %reduce-scatter.55.cloned.1.call-done = f32[384,1120]{0,1:T(8,128)} async-done(((f32[1536,1120]{0,1:T(8,128)}), f32[384,1120]{0,1:T(8,128)}) %reduce-scatter.55.cloned.1.call-update) | async-done | bytes 1720336 | tf_op jit(solution)/shard_map/reduce_scatter | solution.py:312
  2166.2 27.6 %reduce-scatter.53.cloned.1.call-done = f32[192,384]{1,0:T(8,128)} async-done(((f32[192,1536]{1,0:T(8,128)}), f32[192,384]{1,0:T(8,128)}) %reduce-scatter.53.cloned.1.call-update) | async-done | bytes 294928 | tf_op jit(solution)/shard_map/reduce_scatter | solution.py:311
  2193.9 31.5 %reduce-scatter.51.cloned.1.call-done = f32[192,384]{1,0:T(8,128)} async-done(((f32[192,1536]{1,0:T(8,128)}), f32[192,384]{1,0:T(8,128)}) %reduce-scatter.51.cloned.1.call-update) | async-done | bytes 294928 | tf_op jit(solution)/shard_map/reduce_scatter | solution.py:311
  2227.3 25.5 %reduce-scatter.83.cloned.1.call-done = f32[32,2]{1,0:T(8,128)} async-done(((f32[128,2]{1,0:T(8,128)}), f32[32,2]{1,0:T(8,128)}) %reduce-scatter.83.cloned.1.call-update) | async-done | bytes 272
  2254.2 32.8 %reduce-scatter.49.cloned.1.call-done = f32[384,256]{1,0:T(8,128)} async-done(((f32[1536,256]{1,0:T(8,128)}), f32[384,256]{1,0:T(8,128)}) %reduce-scatter.49.cloned.1.call-update) | async-done | bytes 393232 | tf_op jit(solution)/shard_map/reduce_scatter | solution.py:309
  2287.0 34.2 %reduce-scatter.47.cloned.1.call-done = f32[384,256]{1,0:T(8,128)} async-done(((f32[1536,256]{1,0:T(8,128)}), f32[384,256]{1,0:T(8,128)}) %reduce-scatter.47.cloned.1.call-update) | async-done | bytes 393232 | tf_op jit(solution)/shard_map/reduce_scatter | solution.py:309
  2323.2 69.9 %reduce-scatter.81.cloned.1.call-done = f32[192,1024]{1,0:T(8,128)} async-done(((f32[1536,1024]{1,0:T(8,128)}), f32[192,1024]{1,0:T(8,128)}) %reduce-scatter.81.cloned.1.call-update) | async-done | bytes 786448
  2405.6 13.6 psum.70
  (432 shorter events, 502.3 us)
Async XLA Ops:
  9.2 253.4 %copy-start.7 = (bf16[192,1024]{0,1:T(8,128)(2,1)}, bf16[192,1024]{0,1:T(8,128)(2,1)S(1)}, u32[]{:S(2)}) copy-start(bf16[192,1024]{0,1:T(8,128)(2,1)S(1)} %copy.169) | copy-start | bytes 1179652
  28.9 249.5 %copy-start.59 = (f32[1,1,192]{2,1,0:T(1,128)}, f32[1,1,192]{2,1,0:T(1,128)S(1)}, u32[]{:S(2)}) copy-start(f32[1,1,192]{2,1,0:T(1,128)S(1)} %get-tuple-element.132) | copy-start | bytes 2308
  28.9 451.8 %copy-start.61 = (f32[1,1,192]{2,1,0:T(1,128)}, f32[1,1,192]{2,1,0:T(1,128)S(1)}, u32[]{:S(2)}) copy-start(f32[1,1,192]{2,1,0:T(1,128)S(1)} %get-tuple-element.131) | copy-start | bytes 2308
  31.9 76.1 %all-to-all-start = ((bf16[8,192,1024]{2,1,0:T(8,128)(2,1)}), bf16[8,192,1024]{2,1,0:T(8,128)(2,1)}, u32[]{:S(2)}, u32[]{:S(2)}) async-start(bf16[8,192,1024]{2,1,0:T(8,128)(2,1)} %stack.70), calls=%async_computation | async-start | bytes 6291456 | tf_op jit(solution)/shard_map/all_to_all | solution.py:21
  36.5 121.0 %all-gather.21.cloned.1.call-start = ((), (), s32[]{:S(2)}) async-start(), calls=%async_computation.38 | async-start | bytes 1179648 | tf_op jit(solution)/shard_map/all_gather | solution.py:175
  164.0 16.1 all-to-all-start.2
  167.6 92.6 %reduce-scatter.67.cloned.1.call-start = ((), (), s32[]{:S(2)}) async-start(), calls=%async_computation.58 | async-start | bytes 7077888
  190.5 98.4 %all-gather.25.cloned.1.call-start = ((), (), s32[]{:S(2)}) async-start(), calls=%async_computation.52 | async-start | bytes 4300800 | tf_op jit(solution)/shard_map/all_gather | solution.py:163
  193.3 172.9 %all-gather.27.cloned.1.call-start = ((), (), s32[]{:S(2)}) async-start(), calls=%async_computation.53 | async-start | bytes 4300800 | tf_op jit(solution)/shard_map/all_gather | solution.py:164
  281.4 76.0 %all-to-all-start.3 = ((bf16[8,192,1024]{2,1,0:T(8,128)(2,1)}), bf16[8,192,1024]{2,1,0:T(8,128)(2,1)}, u32[]{:S(2)}, u32[]{:S(2)}) async-start(bf16[8,192,1024]{2,1,0:T(8,128)(2,1)} %stack.71), calls=%async_computation.3 | async-start | bytes 6291456 | tf_op jit(solution)/shard_map/all_to_all | solution.py:21
  285.9 91.5 %all-gather.29.cloned.1.call-start = ((), (), s32[]{:S(2)}) async-start(), calls=%async_computation.54 | async-start | bytes 4300800 | tf_op jit(solution)/shard_map/all_gather | solution.py:165
  288.8 173.7 %reduce-scatter.69.cloned.1.call-start = ((), (), s32[]{:S(2)}) async-start(), calls=%async_computation.59 | async-start | bytes 7077888
  466.4 246.1 %copy-start.6 = (f32[192,1024]{0,1:T(8,128)}, f32[192,1024]{0,1:T(8,128)S(1)}, u32[]{:S(2)}) copy-start(f32[192,1024]{0,1:T(8,128)S(1)} %get-tuple-element.89) | copy-start | bytes 2359300
  483.8 76.0 %all-to-all-start.4 = ((bf16[8,192,1024]{2,1,0:T(8,128)(2,1)}), bf16[8,192,1024]{2,1,0:T(8,128)(2,1)}, u32[]{:S(2)}, u32[]{:S(2)}) async-start(bf16[8,192,1024]{2,1,0:T(8,128)(2,1)} %stack.72), calls=%async_computation.4 | async-start | bytes 6291456 | tf_op jit(solution)/shard_map/all_to_all | solution.py:21
  488.3 121.7 %all-gather.23.cloned.1.call-start = ((), (), s32[]{:S(2)}) async-start(), calls=%async_computation.39 | async-start | bytes 1179648 | tf_op jit(solution)/shard_map/all_gather | solution.py:175
  615.7 16.1 all-to-all-start.6
  619.3 91.7 %reduce-scatter.71.cloned.1.call-start = ((), (), s32[]{:S(2)}) async-start(), calls=%async_computation.60 | async-start | bytes 7077888
  642.1 170.4 %all-gather.33.cloned.1.call-start = ((), (), s32[]{:S(2)}) async-start(), calls=%async_computation.56 | async-start | bytes 4300800 | tf_op jit(solution)/shard_map/all_gather | solution.py:164
  728.9 76.1 %all-to-all-start.7 = ((bf16[8,192,1024]{2,1,0:T(8,128)(2,1)}), bf16[8,192,1024]{2,1,0:T(8,128)(2,1)}, u32[]{:S(2)}, u32[]{:S(2)}) async-start(bf16[8,192,1024]{2,1,0:T(8,128)(2,1)} %stack.73), calls=%async_computation.7 | async-start | bytes 6291456 | tf_op jit(solution)/shard_map/all_to_all | solution.py:21
  733.5 87.9 %all-gather.31.cloned.1.call-start = ((), (), s32[]{:S(2)}) async-start(), calls=%async_computation.55 | async-start | bytes 4300800 | tf_op jit(solution)/shard_map/all_gather | solution.py:163
  807.1 76.0 %all-to-all-start.8 = ((bf16[8,192,1024]{2,1,0:T(8,128)(2,1)}), bf16[8,192,1024]{2,1,0:T(8,128)(2,1)}, u32[]{:S(2)}, u32[]{:S(2)}) async-start(bf16[8,192,1024]{2,1,0:T(8,128)(2,1)} %stack.74), calls=%async_computation.8 | async-start | bytes 6291456 | tf_op jit(solution)/shard_map/all_to_all | solution.py:21
  811.5 50.1 %all-gather.35.cloned.1.call-start = ((), (), s32[]{:S(2)}) async-start(), calls=%async_computation.57 | async-start | bytes 4300800 | tf_op jit(solution)/shard_map/all_gather | solution.py:165
  812.3 169.8 %reduce-scatter.75.cloned.1.call-start = ((), (), s32[]{:S(2)}) async-start(), calls=%async_computation.62 | async-start | bytes 7077888
  913.2 139.6 %reduce-scatter.73.cloned.1.call-start = ((), (), s32[]{:S(2)}) async-start(), calls=%async_computation.61 | async-start | bytes 7077888
  1134.5 15.9 all-to-all-start.10
  1138.0 64.7 %reduce-scatter.43.cloned.1.call-start = ((), (), s32[]{:S(2)}) async-start(), calls=%async_computation.40 | async-start | bytes 2359296 | tf_op jit(solution)/shard_map/reduce_scatter | solution.py:295
  1167.7 139.0 %reduce-scatter.77.cloned.1.call-start = ((), (), s32[]{:S(2)}) async-start(), calls=%async_computation.63 | async-start | bytes 7077888
  1238.1 261.9 %reduce-scatter.79.cloned.1.call-start = ((), (), s32[]{:S(2)}) async-start(), calls=%async_computation.64 | async-start | bytes 7077888
  1601.2 15.9 all-to-all-start.14
  1604.6 96.6 %reduce-scatter.45.cloned.1.call-start = ((), (), s32[]{:S(2)}) async-start(), calls=%async_computation.41 | async-start | bytes 2359296 | tf_op jit(solution)/shard_map/reduce_scatter | solution.py:295
  1634.4 109.0 %reduce-scatter.85.cloned.1.call-start = ((), (), s32[]{:S(2)}) async-start(), calls=%async_computation.67 | async-start | bytes 81920
  1636.4 136.7 %reduce-scatter.65.cloned.1.call-start = ((), (), s32[]{:S(2)}) async-start(), calls=%async_computation.51 | async-start | bytes 8601600 | tf_op jit(solution)/shard_map/reduce_scatter | solution.py:314
  1645.6 205.3 %reduce-scatter.63.cloned.1.call-start = ((), (), s32[]{:S(2)}) async-start(), calls=%async_computation.50 | async-start | bytes 8601600 | tf_op jit(solution)/shard_map/reduce_scatter | solution.py:314
  1654.9 273.9 %reduce-scatter.61.cloned.1.call-start = ((), (), s32[]{:S(2)}) async-start(), calls=%async_computation.49 | async-start | bytes 8601600 | tf_op jit(solution)/shard_map/reduce_scatter | solution.py:313
  1664.7 341.9 %reduce-scatter.59.cloned.1.call-start = ((), (), s32[]{:S(2)}) async-start(), calls=%async_computation.48 | async-start | bytes 8601600 | tf_op jit(solution)/shard_map/reduce_scatter | solution.py:313
  1674.0 410.5 %reduce-scatter.57.cloned.1.call-start = ((), (), s32[]{:S(2)}) async-start(), calls=%async_computation.47 | async-start | bytes 8601600 | tf_op jit(solution)/shard_map/reduce_scatter | solution.py:312
  1683.3 479.0 %reduce-scatter.55.cloned.1.call-start = ((), (), s32[]{:S(2)}) async-start(), calls=%async_computation.46 | async-start | bytes 8601600 | tf_op jit(solution)/shard_map/reduce_scatter | solution.py:312
  1692.7 501.1 %reduce-scatter.53.cloned.1.call-start = ((), (), s32[]{:S(2)}) async-start(), calls=%async_computation.45 | async-start | bytes 1474560 | tf_op jit(solution)/shard_map/reduce_scatter | solution.py:311
  1696.0 529.3 %reduce-scatter.51.cloned.1.call-start = ((), (), s32[]{:S(2)}) async-start(), calls=%async_computation.44 | async-start | bytes 1474560 | tf_op jit(solution)/shard_map/reduce_scatter | solution.py:311
  1700.4 552.4 %reduce-scatter.83.cloned.1.call-start = ((), (), s32[]{:S(2)}) async-start(), calls=%async_computation.66 | async-start | bytes 81920
  1722.2 564.8 %reduce-scatter.49.cloned.1.call-start = ((), (), s32[]{:S(2)}) async-start(), calls=%async_computation.43 | async-start | bytes 1966080 | tf_op jit(solution)/shard_map/reduce_scatter | solution.py:309
  1726.5 594.6 %reduce-scatter.47.cloned.1.call-start = ((), (), s32[]{:S(2)}) async-start(), calls=%async_computation.42 | async-start | bytes 1966080 | tf_op jit(solution)/shard_map/reduce_scatter | solution.py:309
  1731.1 662.0 %reduce-scatter.81.cloned.1.call-start = ((), (), s32[]{:S(2)}) async-start(), calls=%async_computation.65 | async-start | bytes 7077888
  2166.2 228.4 %copy-start.8 = (bf16[192,1024]{0,1:T(8,128)(2,1)S(1)}, bf16[192,1024]{0,1:T(8,128)(2,1)}, u32[]{:S(2)}) copy-start(bf16[192,1024]{0,1:T(8,128)(2,1)} %copy-done.7) | copy-start | bytes 1179652
  2166.2 228.4 %copy-start.52 = (f32[1024]{0:T(1024)S(1)}, f32[1024]{0:T(1024)}, u32[]{:S(2)}) copy-start(f32[1024]{0:T(1024)} %copy-done.51) | copy-start | bytes 12292
  2166.2 228.4 %copy-start.64 = (f32[1,1,192]{2,1,0:T(1,128)S(1)}, f32[1,1,192]{2,1,0:T(1,128)}, u32[]{:S(2)}) copy-start(f32[1,1,192]{2,1,0:T(1,128)} %copy-done.63) | copy-start | bytes 2308
  2166.2 228.9 %copy-start.69 = (f32[192]{0:T(256)S(1)}, f32[192]{0:T(256)}, u32[]{:S(2)}) copy-start(f32[192]{0:T(256)} %get-tuple-element.72) | copy-start | bytes 2308
  2166.2 253.0 %copy-start.65 = (f32[1024]{0:T(1024)S(1)}, f32[1024]{0:T(1024)}, u32[]{:S(2)}) copy-start(f32[1024]{0:T(1024)} %get-tuple-element.122) | copy-start | bytes 12292
  (73 other events, 1444.6 us)
Sparse Core Ops, SparseCore 0:
  134.6 22.7 all-gather.20
  190.6 69.5 reduce-scatter.66
  393.7 68.7 reduce-scatter.68
  587.0 22.8 all-gather.22
  642.3 68.7 reduce-scatter.70
  913.3 68.7 reduce-scatter.74
  984.4 68.3 reduce-scatter.72
  1167.8 34.7 reduce-scatter.42
  1238.2 68.4 reduce-scatter.76
  1431.4 68.6 reduce-scatter.78
  1634.5 34.8 reduce-scatter.44
  1672.6 22.4 reduce-scatter.84
  1698.1 74.9 reduce-scatter.64
  1776.0 74.9 reduce-scatter.62
  1853.8 74.9 reduce-scatter.60
  1931.6 74.9 reduce-scatter.58
  2009.4 74.9 reduce-scatter.56
  2087.3 74.9 reduce-scatter.54
  2165.1 28.6 reduce-scatter.52
  2196.6 28.6 reduce-scatter.50
  2228.7 24.0 reduce-scatter.82
  2255.8 31.1 reduce-scatter.48
  2290.0 31.1 reduce-scatter.46
  2323.3 69.7 reduce-scatter.80
Sparse Core Ops, SparseCore 1:
  193.4 45.9 all-gather.24
  241.0 46.0 all-gather.26
  288.9 47.5 all-gather.28
  644.7 45.0 all-gather.32
  736.7 47.5 all-gather.30
  814.1 47.5 all-gather.34
